TPU v7x, 128 devices: a whole 4x4x4 slice. The times are simulated.
128 devices in a mesh: pts: 64 (over z, x, y), grp: 2 (over core).
Axes of the slice: x: 4, y: 4, z: 4, core: 2. Of those that a mesh axis runs over, the one named last changes fastest.
Arguments:
- cam_jac: float32 [18, 1048576], P(None, ('pts', 'grp')), may hold values from -0.25 to 0.25
- pt_jac: float32 [6, 1048576], P(None, ('pts', 'grp')), may hold values from -6 to 6
- resid: float32 [2, 1048576], P(None, ('pts', 'grp')), may hold values from -102 to 102
- obs_point: int32 [1048576], P(('pts', 'grp')), may hold values from 0 to 262143, as said below
- obs_camera: int32 [1048576], P(('pts', 'grp')), may hold values from 0 to 2047
- camera_slot: int32 [2048], replicated, may hold values from 0 to 2047, each once
Outputs:
- cam_inverse: float32 [81, 2048], P(None, ('pts', 'grp'))
- precond: float32 [9, 1048576], P(None, ('pts', 'grp'))
Inputs may be any that keep to these rules, and one draw needn't show every extreme that they name: `obs_point`: observation o names a point of block o // 8192, from (o // 8192) * 2048 to (o // 8192 + 1) * 2048 - 1; within each block of 8192 observations the point number never falls and rises by at most 1 from one observation to the next, and the block's first observation names the block's first point. Each slot appears once; camera c is owned by device camera_slot[c] // 16 of the joined axes pts+grp.
All inputs are finite; a program needn't handle non-finite values.
Results may differ from a plain program's by a relative error of at most 0.0003.
Values sent between devices are 32-bit elements; how exact they have to be, the bound alone decides.
A program may use at most 64 MiB of HBM per device.

v0:
```python
import jax
import jax.numpy as jnp
from jax import lax
from jax.sharding import PartitionSpec as P

PTS_DEV = 2048
DAMP = 1.0
SPAN = 512


def split_up(value, dim, length):
    lengths = value.shape
    parts = value.reshape(*lengths[:dim], length, lengths[dim] // length, *lengths[dim + 1 :])
    return jnp.moveaxis(parts, dim, 0)


def sum_at_owner(value, axis, dim):
    length = lax.axis_size(axis)
    parts = lax.all_to_all(split_up(value, dim, length), axis, 0, 0, tiled=True)
    return jnp.sum(parts, axis=0)


def lower_pairs():
    return [(row_at, col_at) for row_at in range(9) for col_at in range(row_at + 1)]


def exact_dot(left, right):
    return jnp.dot(left, right, precision=lax.Precision.HIGHEST, preferred_element_type=jnp.float32)


def point_table(pt_jac, resid, local_point, npoints):
    entries = []
    for row_at in range(3):
        for col_at in range(row_at, 3):
            entries.append(
                pt_jac[row_at] * pt_jac[col_at] + pt_jac[3 + row_at] * pt_jac[3 + col_at]
            )
    for row_at in range(3):
        entries.append(pt_jac[row_at] * resid[0] + pt_jac[3 + row_at] * resid[1])
    stacked = jnp.stack(entries, 0)
    count = stacked.shape[1] // SPAN
    pieces = jnp.moveaxis(stacked.reshape(9, count, SPAN), 1, 0)
    point_rows = local_point.reshape(count, SPAN)
    firsts = point_rows[:, 0]
    window_ids = jnp.arange(SPAN, dtype=jnp.int32)

    def add_block(carry, inputs):
        piece, points, first = inputs
        onehot = (points[:, None] - first == window_ids[None, :]).astype(jnp.float32)
        window = lax.dynamic_slice_in_dim(carry, first, SPAN, 1)
        carry = lax.dynamic_update_slice_in_dim(carry, window + exact_dot(piece, onehot), first, 1)
        return (carry, None)

    sums, unused = lax.scan(
        add_block, jnp.zeros((9, npoints + SPAN), jnp.float32), (pieces, point_rows, firsts)
    )
    v00 = sums[0] + DAMP
    v01 = sums[1]
    v02 = sums[2]
    v11 = sums[3] + DAMP
    v12 = sums[4]
    v22 = sums[5] + DAMP
    c00 = v11 * v22 - v12 * v12
    c01 = v02 * v12 - v01 * v22
    c02 = v01 * v12 - v02 * v11
    c11 = v00 * v22 - v02 * v02
    c12 = v01 * v02 - v00 * v12
    c22 = v00 * v11 - v01 * v01
    determ = v00 * c00 + v01 * c01 + v02 * c02
    i00 = c00 / determ
    i01 = c01 / determ
    i02 = c02 / determ
    i11 = c11 / determ
    i12 = c12 / determ
    i22 = c22 / determ
    w_zero = i00 * sums[6] + i01 * sums[7] + i02 * sums[8]
    w_one = i01 * sums[6] + i11 * sums[7] + i12 * sums[8]
    w_two = i02 * sums[6] + i12 * sums[7] + i22 * sums[8]
    table = jnp.stack([i00, i01, i02, i11, i12, i22, w_zero, w_one, w_two], 0)

    def pick_block(carry, inputs):
        points, first = inputs
        onehot = (points[:, None] - first == window_ids[None, :]).astype(jnp.float32)
        window = lax.dynamic_slice_in_dim(table, first, SPAN, 1)
        return (carry, exact_dot(window, onehot.T))

    unused, picked = lax.scan(pick_block, 0, (point_rows, firsts))
    return jnp.moveaxis(picked, 0, 1).reshape(9, count * SPAN)


def obs_terms(cam_jac, pt_jac, resid, point_rows, pairs):
    i00, i01, i02, i11, i12, i22 = [point_rows[pos] for pos in range(6)]
    weights = [point_rows[6], point_rows[7], point_rows[8]]
    vinv = ((i00, i01, i02), (i01, i11, i12), (i02, i12, i22))
    prow = [[pt_jac[3 * rowp + inner] for inner in range(3)] for rowp in range(2)]
    usage = [
        [
            vinv[outer][0] * prow[rowp][0]
            + vinv[outer][1] * prow[rowp][1]
            + vinv[outer][2] * prow[rowp][2]
            for outer in range(3)
        ]
        for rowp in range(2)
    ]
    proj_zz = prow[0][0] * usage[0][0] + prow[0][1] * usage[0][1] + prow[0][2] * usage[0][2]
    proj_zo = prow[0][0] * usage[1][0] + prow[0][1] * usage[1][1] + prow[0][2] * usage[1][2]
    proj_oo = prow[1][0] * usage[1][0] + prow[1][1] * usage[1][1] + prow[1][2] * usage[1][2]
    keep = ((1.0 - proj_zz, -proj_zo), (-proj_zo, 1.0 - proj_oo))
    shifted = [
        resid[rowp]
        - (prow[rowp][0] * weights[0] + prow[rowp][1] * weights[1] + prow[rowp][2] * weights[2])
        for rowp in range(2)
    ]
    reduced = jnp.stack(
        [cam_jac[col_at] * shifted[0] + cam_jac[9 + col_at] * shifted[1] for col_at in range(9)], 0
    )
    mixed = [
        [
            keep[rowp][0] * cam_jac[col_at] + keep[rowp][1] * cam_jac[9 + col_at]
            for col_at in range(9)
        ]
        for rowp in range(2)
    ]
    terms = jnp.stack(
        [
            cam_jac[row_at] * mixed[0][col_at] + cam_jac[9 + row_at] * mixed[1][col_at]
            for row_at, col_at in pairs
        ],
        0,
    )
    return (terms, reduced)


def chol_inverse(rows, pairs):
    entry = {pair: rows[pos] for pos, pair in enumerate(pairs)}
    factor = {}
    for col_at in range(9):
        diag = entry[col_at, col_at] + DAMP
        for inner in range(col_at):
            diag = diag - factor[col_at, inner] * factor[col_at, inner]
        root = jnp.sqrt(diag)
        factor[col_at, col_at] = root
        for row_at in range(col_at + 1, 9):
            value = entry[row_at, col_at]
            for inner in range(col_at):
                value = value - factor[row_at, inner] * factor[col_at, inner]
            factor[row_at, col_at] = value / root
    solved = {}
    for col_at in range(9):
        solved[col_at, col_at] = 1.0 / factor[col_at, col_at]
        for row_at in range(col_at + 1, 9):
            value = factor[row_at, col_at] * solved[col_at, col_at]
            for inner in range(col_at + 1, row_at):
                value = value + factor[row_at, inner] * solved[inner, col_at]
            solved[row_at, col_at] = -value / factor[row_at, row_at]
    result = {}
    for row_at in range(9):
        for col_at in range(row_at + 1):
            value = solved[row_at, row_at] * solved[row_at, col_at]
            for inner in range(row_at + 1, 9):
                value = value + solved[inner, row_at] * solved[inner, col_at]
            result[row_at, col_at] = value
            result[col_at, row_at] = value
    return jnp.stack([result[row_at, col_at] for row_at in range(9) for col_at in range(9)], 0)


def apply_inverse(picked, reduced, locate):
    outputs = []
    for row_at in range(9):
        value = picked[locate[row_at, 0]] * reduced[0]
        for col_at in range(1, 9):
            value = value + picked[locate[row_at, col_at]] * reduced[col_at]
        outputs.append(value)
    return jnp.stack(outputs, 0)


def shards(cam_jac, pt_jac, resid, obs_point, obs_camera, camera_slot):
    cameras = camera_slot.shape[0]
    owned_count = cameras // lax.axis_size(("pts", "grp"))
    local_point = obs_point - lax.axis_index(("pts", "grp")) * PTS_DEV
    rows = point_table(pt_jac, resid, local_point, PTS_DEV)
    pairs = lower_pairs()
    terms, reduced = obs_terms(cam_jac, pt_jac, resid, rows, pairs)
    width = len(pairs)
    camera_of_slot = (
        jnp.zeros((cameras,), jnp.int32).at[camera_slot].set(jnp.arange(cameras, dtype=jnp.int32))
    )
    count = terms.shape[1] // SPAN
    term_blocks = jnp.moveaxis(terms.reshape(width, count, SPAN), 1, 0)
    camera_blocks = obs_camera.reshape(count, SPAN)

    def add_cameras(carry, inputs):
        piece, named = inputs
        onehot = (named[:, None] == camera_of_slot[None, :]).astype(jnp.bfloat16)
        return (carry + exact_dot(piece, onehot.astype(jnp.float32)), None)

    partial_value, unused = lax.scan(
        add_cameras, jnp.zeros((width, cameras), jnp.float32), (term_blocks, camera_blocks)
    )
    split = partial_value.reshape(width, lax.axis_size("pts"), lax.axis_size("grp"), owned_count)
    split = sum_at_owner(split, "grp", 2)
    split = sum_at_owner(split, "pts", 1)
    owned = split.reshape(width, owned_count)
    inverse = chol_inverse(owned, pairs)
    outgoing = jnp.stack([inverse[row_at * 9 + col_at] for row_at, col_at in pairs], 0)
    table = lax.all_gather(outgoing, ("pts", "grp"), axis=1, tiled=True)

    def pick_cameras(carry, named):
        onehot = (named[:, None] == camera_of_slot[None, :]).astype(jnp.bfloat16)
        return (carry, exact_dot(table, onehot.astype(jnp.float32).T))

    unused, picked = lax.scan(pick_cameras, 0, camera_blocks)
    picked = jnp.moveaxis(picked, 0, 1).reshape(width, count * SPAN)
    position = {pair: pos for pos, pair in enumerate(pairs)}
    locate = {}
    for row_at in range(9):
        for col_at in range(9):
            if (row_at, col_at) in position:
                locate[row_at, col_at] = position[row_at, col_at]
            else:
                locate[row_at, col_at] = position[col_at, row_at]
    precond = apply_inverse(picked, reduced, locate)
    return (inverse, precond)


def solution(mesh):
    in_specs = (
        P(None, ("pts", "grp")),
        P(None, ("pts", "grp")),
        P(None, ("pts", "grp")),
        P(("pts", "grp")),
        P(("pts", "grp")),
        P(),
    )
    out_specs = (P(None, ("pts", "grp")), P(None, ("pts", "grp")))
    return jax.shard_map(shards, mesh=mesh, in_specs=in_specs, out_specs=out_specs, check_vma=False)
```

profile of v0, /device:TPU:1, one launch (start us, length us, event | category | flops | bytes accessed | tf_op | source)
XLA Modules:
  0.0 349.4 jit_solution(5146475019787182314)
XLA Ops:
  1.6 1.9 multiply_add_fusion.87
  3.5 2.0 multiply_add_fusion.82
  6.0 70.7 %while.44 = (s32[]{:T(128)}, f32[9,2560]{1,0:T(8,128)S(1)}, s32[16]{0:T(128)S(1)}, f32[16,9,512]{2,1,0:T(8,128)S(1)}, s32[16,512]{1,0:T(8,128)S(1)}, /*index=5*/s32[]{:T(128)}, s32[]{:T(128)}, s32[]{:T(128)}) while((s32[]{:T(128)}, f32[9,2560]{1,0:T(8,128)S(1)}, s32[16]{0:T(128)S(1)}, f32[16,9,512]{2,1,0:T(8,128)S(1)}, ...), condition=%wide.region_1.2_spmd.clone, body=%wide.region_0.1_spmd.clone.sunk | while | flops 28578820 | bytes 127135 | solution.py:54
  77.1 64.2 %while.45 = (s32[]{:T(128)}, f32[16,9,512]{2,1,0:T(8,128)S(1)}, s32[16]{0:T(128)S(1)}, f32[9,2560]{1,0:T(8,128)S(1)}, s32[16,512]{1,0:T(8,128)S(1)}, /*index=5*/s32[]{:T(128)}, s32[]{:T(128)}, s32[]{:T(128)}) while((s32[]{:T(128)}, f32[16,9,512]{2,1,0:T(8,128)S(1)}, s32[16]{0:T(128)S(1)}, f32[9,2560]{1,0:T(8,128)S(1)}, ...), condition=%wide.region_3.4_spmd.clone, body=%wide.region_2.3_spmd.clone.sunk | while | flops 28574212 | bytes 71835 | solution.py:87
  144.5 8.2 %scatter_custom_fusion = s32[2048]{0:T(1024)S(1)} fusion(s32[2048]{0:T(1024)S(1)} %compare_select_fusion, s32[2048]{0:T(1024)S(1)} %iota.10, s32[]{:T(128)} %copy.541), kind=kCustom, calls=%fused_computation.145 | custom fusion | bytes 8196 | tf_op jit(solution)/shard_map/scatter | solution.py:186
  153.7 1.1 multiply_add_fusion.36
  158.0 6.3 %stack.335 = f32[45,16,512]{2,0,1:T(8,128)S(1)} concatenate(f32[1,16,512]{2,0,1:T(1,128)} %bitcast.291, f32[1,16,512]{2,0,1:T(1,128)} %bitcast.290, f32[1,16,512]{2,0,1:T(1,128)} %bitcast.270, f32[1,16,512]{2,0,1:T(1,128)} %bitcast.289, f32[1,16,512]{2,0,1:T(1,128)S(1)} %bitcast.269, f32[1,16,512]{2,0,1:T(1,128)} %bitcast.276, f32[1,16,512]{2,0,1:T(1,128)} %bitcast.288, ...), dimensions={0} | concatenate | bytes 2949120 | tf_op jit(solution)/shard_map/stack | solution.py:124
  164.3 38.5 %while.46 = (s32[]{:T(128)}, f32[45,2048]{1,0:T(8,128)S(1)}, f32[16,45,512]{2,1,0:T(8,128)S(1)}, s32[16,512]{1,0:T(8,128)}, s32[2048]{0:T(1024)S(1)}, /*index=5*/s32[]{:T(128)}, s32[]{:T(128)}) while((s32[]{:T(128)}, f32[45,2048]{1,0:T(8,128)S(1)}, f32[16,45,512]{2,1,0:T(8,128)S(1)}, s32[16,512]{1,0:T(8,128)}, s32[2048]{0:T(1024)S(1)}, ...), condition=%wide.region_6.7_spmd.clone, body=%wide.region_5.6_spmd.clone.sunk | while | flops 567463936 | bytes 874599 | solution.py:197
  165.0 1.7 fusion.91
  167.4 1.7 fusion.91
  169.8 1.7 fusion.91
  172.3 1.7 fusion.91
  174.7 1.7 fusion.91
  177.1 1.7 fusion.91
  179.5 1.7 fusion.91
  181.9 1.7 fusion.91
  184.3 1.7 fusion.91
  186.7 1.7 fusion.91
  189.1 1.7 fusion.91
  191.5 1.7 fusion.91
  193.9 1.7 fusion.91
  196.3 1.7 fusion.91
  198.8 1.7 fusion.91
  201.2 1.7 fusion.91
  204.5 5.0 %all_to_all.10 = f32[2,1,46080]{2,1,0:T(1,128)S(1)} all-to-all(f32[2,1,46080]{2,1,0:T(1,128)S(1)} %reshape.4789), channel_id=1, replica_groups=mesh['pts'=64,'grp'=2] {'grp'}, dimensions={0} | all-to-all | bytes 737280 | tf_op jit(solution)/shard_map/all_to_all | solution.py:19
  210.0 1.8 reduce.4
  212.8 1.2 reshape.4791
  214.0 11.3 %all-to-all-start.1 = ((f32[64,1,720]{2,1,0:T(1,128)}), f32[64,1,720]{2,1,0:T(1,128)S(1)}, u32[]{:S(2)}, u32[]{:S(2)}) async-start(f32[64,1,720]{2,1,0:T(1,128)} %reshape.4791), calls=%async_computation.1 | async-start | bytes 393216 | tf_op jit(solution)/shard_map/all_to_all | solution.py:19
  225.5 8.6 %all-to-all-done.1 = f32[64,1,720]{2,1,0:T(1,128)S(1)} async-done(((f32[64,1,720]{2,1,0:T(1,128)}), f32[64,1,720]{2,1,0:T(1,128)S(1)}, u32[]{:S(2)}, u32[]{:S(2)}) %all-to-all-start.1) | async-done | bytes 184352 | tf_op jit(solution)/shard_map/all_to_all | solution.py:19
  245.2 35.8 %all_gather.3 = f32[45,2048]{0,1:T(8,128)S(1)} all-gather(f32[45,16]{0,1:T(8,128)S(1)} %stack.337), channel_id=1, replica_groups=mesh['pts'=64,'grp'=2] {'pts','grp'}, dimensions={1}, use_global_device_ids=true | all-gather | bytes 371520 | tf_op jit(solution)/shard_map/all_gather | solution.py:206
  282.0 61.7 %while.43 = (s32[]{:T(128)}, f32[16,45,512]{2,1,0:T(8,128)S(1)}, s32[16,512]{1,0:T(8,128)}, s32[2048]{0:T(1024)S(1)}, f32[45,2048]{1,0:T(8,128)}, /*index=5*/s32[]{:T(128)}) while((s32[]{:T(128)}, f32[16,45,512]{2,1,0:T(8,128)S(1)}, s32[16,512]{1,0:T(8,128)}, s32[2048]{0:T(1024)S(1)}, f32[45,2048]{1,0:T(8,128)}, /*index=5*/s32[]{:T(128)}) %tuple.423), condition=%wide.region_10.11_spmd, body=%wide.region_9.10_spmd.sunk | while | flops 567279616 | bytes 481365 | solution.py:212
  282.7 3.1 fusion.85
  286.6 3.1 fusion.85
  290.4 3.1 fusion.85
  294.3 3.1 fusion.85
  298.2 3.1 fusion.85
  302.0 3.1 fusion.85
  305.9 3.1 fusion.85
  309.7 3.1 fusion.85
  313.6 3.1 fusion.85
  317.4 3.1 fusion.85
  321.3 3.1 fusion.85
  325.2 3.1 fusion.85
  329.0 3.1 fusion.85
  332.9 3.1 fusion.85
  336.7 3.1 fusion.85
  340.6 3.1 fusion.85
  347.5 1.8 stack.338
  (320 shorter events, 120.7 us)
Async XLA Ops:
  76.7 65.5 %copy-start = (f32[18,8192]{1,0:T(8,128)S(1)}, f32[18,8192]{1,0:T(8,128)}, u32[]{:S(2)}) copy-start(f32[18,8192]{1,0:T(8,128)} %param.14) | copy-start | bytes 1769476
  76.7 65.5 %copy-start.1 = (f32[6,8192]{1,0:T(8,128)S(1)}, f32[6,8192]{1,0:T(8,128)}, u32[]{:S(2)}) copy-start(f32[6,8192]{1,0:T(8,128)} %param.15) | copy-start | bytes 589828
  141.3 2.5 copy-start.7
  141.3 2.5 copy-start.6
  212.3 13.0 %copy-start.2 = (f32[2,8192]{1,0:T(2,128)S(1)}, f32[2,8192]{1,0:T(2,128)}, u32[]{:S(2)}) copy-start(f32[2,8192]{1,0:T(2,128)} %param.16) | copy-start | bytes 196612
  212.3 13.0 %copy-start.3 = (f32[1,16,512]{2,0,1:T(1,128)S(1)}, f32[1,16,512]{2,0,1:T(1,128)}, u32[]{:S(2)}) copy-start(f32[1,16,512]{2,0,1:T(1,128)} %get-tuple-element.485) | copy-start | bytes 98308
  212.3 13.0 %copy-start.4 = (f32[1,16,512]{2,0,1:T(1,128)S(1)}, f32[1,16,512]{2,0,1:T(1,128)}, u32[]{:S(2)}) copy-start(f32[1,16,512]{2,0,1:T(1,128)} %get-tuple-element.486) | copy-start | bytes 98308
  212.4 13.0 %copy-start.5 = (f32[1,16,512]{2,0,1:T(1,128)S(1)}, f32[1,16,512]{2,0,1:T(1,128)}, u32[]{:S(2)}) copy-start(f32[1,16,512]{2,0,1:T(1,128)} %get-tuple-element.487) | copy-start | bytes 98308
  214.0 20.2 %all-to-all-start.1 = ((f32[64,1,720]{2,1,0:T(1,128)}), f32[64,1,720]{2,1,0:T(1,128)S(1)}, u32[]{:S(2)}, u32[]{:S(2)}) async-start(f32[64,1,720]{2,1,0:T(1,128)} %reshape.4791), calls=%async_computation.1 | async-start | bytes 393216 | tf_op jit(solution)/shard_map/all_to_all | solution.py:19
where the time goes:
time: 354 us; the launch traced here: 349 us
  matrix products  93.8 us (26%)
  local copies, waits for them, and re-layouts  87.4 us (25%)
  loops' own time  66.1 us (19%)
  blocking collectives  40.8 us (12%)
  other arithmetic  40.1 us (11%)
  starting transfers between devices  11.3 us (3%)
  waiting for transfers between devices  8.62 us (2%)
    dot_general x64, matrix products, exact_dot(): jnp.dot(left, right, precision=lax.Precision.HIGHEST, preferred_element_t...  93.8 us
    dynamic_slice x64, local copies, waits for them, and re-layouts, point_table(): lax.scan(add_block, jnp.zeros((9, npoints + SPAN), jnp.float32), (pieces,...  44.2 us
    all_gather x1, blocking collectives, shards(): table = lax.all_gather(outgoing, ('pts', 'grp'), axis=1, tiled=True)  35.8 us
    another operation x1, loops' own time, point_table(): lax.scan(add_block, jnp.zeros((9, npoints + SPAN), jnp.float32), (pieces,...  32.9 us
    another operation x1, loops' own time, point_table(): unused, picked = lax.scan(pick_block, 0, (point_rows, firsts))  32.5 us
    all_to_all x1, starting transfers between devices, sum_at_owner(): parts = lax.all_to_all(split_up(value, dim, length), axis, 0, 0, tiled=True)  11.3 us
    sub x16, other arithmetic, add_block(): points[:, None] - first == window_ids[None, :]  10.9 us
    sub x16, other arithmetic, pick_block(): points[:, None] - first == window_ids[None, :]  10.9 us
  transfers between devices with their start and end apart: 1, of which 1 were waited for; matrix products, arithmetic and copies ran while one was open for 0% of the time, Pallas kernels for 0%

commit v1 on v0

--- a/solution.py
+++ b/solution.py
@@ -203,7 +203,8 @@
     owned = split.reshape(width, owned_count)
     inverse = chol_inverse(owned, pairs)
     outgoing = jnp.stack([inverse[row_at * 9 + col_at] for row_at, col_at in pairs], 0)
-    table = lax.all_gather(outgoing, ("pts", "grp"), axis=1, tiled=True)
+    repeated = jnp.stack([outgoing] * lax.axis_size(("pts", "grp")))
+    table = jnp.concatenate(lax.all_to_all(repeated, ("pts", "grp"), 0, 0), axis=1)
 
     def pick_cameras(carry, named):
         onehot = (named[:, None] == camera_of_slot[None, :]).astype(jnp.bfloat16)

time: 354 us -> 334 us (0.944)
  blocking collectives: 40.8 us -> 25 us
  local copies, waits for them, and re-layouts: 87.4 us -> 96.7 us
  starting transfers between devices: 11.3 us -> 5.28 us
  matrix products: 93.8 us -> 88.1 us
  loops' own time: 66.1 us -> 62.3 us
    all_gather x1 -> x0, blocking collectives: 35.8 us -> none  [shards(): table = lax.all_gather(outgoing, ('pts', 'grp'), axis=1, tiled=True)]
    all_to_all x1 -> x2, blocking collectives: 5.03 us -> 25 us  [sum_at_owner(): parts = lax.all_to_all(split_up(value, dim, length), axis, 0, 0, tiled=True)]
    slice x2, local copies, waits for them, and re-layouts: 1.12 us -> 7.2 us  [apply_inverse(): value = value + picked[locate[row_at, col_at]] * reduced[col_at]]
    all_to_all x1, starting transfers between devices: 11.3 us -> 5.28 us  [shards(): lax.all_to_all(repeated, ('pts', 'grp'), 0, 0)]
    dot_general x64, matrix products: 93.8 us -> 88.1 us  [exact_dot(): jnp.dot(left, right, precision=lax.Precision.HIGHEST, preferred_element_t...]
    unnamed x67 -> x70, local copies, waits for them, and re-layouts: 6.46 us -> 8.65 us
where the time goes in v1:
time: 334 us; the launch traced here: 330 us
  local copies, waits for them, and re-layouts  96.7 us (29%)
  matrix products  88.1 us (26%)
  loops' own time  62.3 us (19%)
  other arithmetic  40.4 us (12%)
  blocking collectives  25 us (7%)
  waiting for transfers between devices  11.1 us (3%)
  starting transfers between devices  5.28 us (2%)
    dot_general x64, matrix products, exact_dot(): jnp.dot(left, right, precision=lax.Precision.HIGHEST, preferred_element_t...  88.1 us
    dynamic_slice x64, local copies, waits for them, and re-layouts, point_table(): lax.scan(add_block, jnp.zeros((9, npoints + SPAN), jnp.float32), (pieces,...  44.3 us
    another operation x1, loops' own time, point_table(): lax.scan(add_block, jnp.zeros((9, npoints + SPAN), jnp.float32), (pieces,...  31.1 us
    another operation x1, loops' own time, point_table(): unused, picked = lax.scan(pick_block, 0, (point_rows, firsts))  30.8 us
    all_to_all x2, blocking collectives, sum_at_owner(): parts = lax.all_to_all(split_up(value, dim, length), axis, 0, 0, tiled=True)  25 us
    all_to_all x1, waiting for transfers between devices, shards(): lax.all_to_all(repeated, ('pts', 'grp'), 0, 0)  11.1 us
    sub x16, other arithmetic, add_block(): points[:, None] - first == window_ids[None, :]  10.3 us
    sub x16, other arithmetic, pick_block(): points[:, None] - first == window_ids[None, :]  10.3 us
  transfers between devices with their start and end apart: 1, of which 1 were waited for; matrix products, arithmetic and copies ran while one was open for 0% of the time, Pallas kernels for 0%

profile of v1, /device:TPU:1, one launch (start us, length us, event | category | flops | bytes accessed | tf_op | source)
XLA Modules:
  0.0 330.2 jit_solution(6855142550073697967)
XLA Ops:
  1.6 1.9 multiply_add_fusion.87
  3.5 2.0 multiply_add_fusion.82
  6.0 68.4 %while.44 = (s32[]{:T(128)}, f32[9,2560]{1,0:T(8,128)S(1)}, s32[16]{0:T(128)S(1)}, f32[16,9,512]{2,1,0:T(8,128)S(1)}, s32[16,512]{1,0:T(8,128)S(1)}, /*index=5*/s32[]{:T(128)}, s32[]{:T(128)}, s32[]{:T(128)}) while((s32[]{:T(128)}, f32[9,2560]{1,0:T(8,128)S(1)}, s32[16]{0:T(128)S(1)}, f32[16,9,512]{2,1,0:T(8,128)S(1)}, ...), condition=%wide.region_1.2_spmd.clone, body=%wide.region_0.1_spmd.clone.sunk | while | flops 28578820 | bytes 127135 | solution.py:54
  74.8 62.0 %while.45 = (s32[]{:T(128)}, f32[16,9,512]{2,1,0:T(8,128)S(1)}, s32[16]{0:T(128)S(1)}, f32[9,2560]{1,0:T(8,128)S(1)}, s32[16,512]{1,0:T(8,128)S(1)}, /*index=5*/s32[]{:T(128)}, s32[]{:T(128)}, s32[]{:T(128)}) while((s32[]{:T(128)}, f32[16,9,512]{2,1,0:T(8,128)S(1)}, s32[16]{0:T(128)S(1)}, f32[9,2560]{1,0:T(8,128)S(1)}, ...), condition=%wide.region_3.4_spmd.clone, body=%wide.region_2.3_spmd.clone.sunk | while | flops 28574212 | bytes 71835 | solution.py:87
  139.9 8.2 %scatter_custom_fusion = s32[2048]{0:T(1024)S(1)} fusion(s32[2048]{0:T(1024)S(1)} %compare_select_fusion, s32[2048]{0:T(1024)S(1)} %iota.10, s32[]{:T(128)} %copy.543), kind=kCustom, calls=%fused_computation.145 | custom fusion | bytes 8196 | tf_op jit(solution)/shard_map/scatter | solution.py:186
  153.4 6.3 %stack.178 = f32[45,16,512]{2,0,1:T(8,128)S(1)} concatenate(f32[1,16,512]{2,0,1:T(1,128)} %bitcast.298, f32[1,16,512]{2,0,1:T(1,128)} %bitcast.297, f32[1,16,512]{2,0,1:T(1,128)} %bitcast.277, f32[1,16,512]{2,0,1:T(1,128)} %bitcast.296, f32[1,16,512]{2,0,1:T(1,128)S(1)} %bitcast.276, f32[1,16,512]{2,0,1:T(1,128)} %bitcast.283, f32[1,16,512]{2,0,1:T(1,128)} %bitcast.295, ...), dimensions={0} | concatenate | bytes 2949120 | tf_op jit(solution)/shard_map/stack | solution.py:124
  159.7 38.5 %while.46 = (s32[]{:T(128)}, f32[45,2048]{1,0:T(8,128)S(1)}, f32[16,45,512]{2,1,0:T(8,128)S(1)}, s32[16,512]{1,0:T(8,128)}, s32[2048]{0:T(1024)S(1)}, /*index=5*/s32[]{:T(128)}, s32[]{:T(128)}) while((s32[]{:T(128)}, f32[45,2048]{1,0:T(8,128)S(1)}, f32[16,45,512]{2,1,0:T(8,128)S(1)}, s32[16,512]{1,0:T(8,128)}, s32[2048]{0:T(1024)S(1)}, ...), condition=%wide.region_6.7_spmd.clone, body=%wide.region_5.6_spmd.clone.sunk | while | flops 567463936 | bytes 874599 | solution.py:197
  160.5 1.7 fusion.91
  162.9 1.7 fusion.91
  165.3 1.7 fusion.91
  167.7 1.7 fusion.91
  170.1 1.7 fusion.91
  172.5 1.7 fusion.91
  174.9 1.7 fusion.91
  177.3 1.7 fusion.91
  179.7 1.7 fusion.91
  182.1 1.7 fusion.91
  184.5 1.7 fusion.91
  187.0 1.7 fusion.91
  194.2 1.7 fusion.91
  196.6 1.7 fusion.91
  199.9 5.0 %all_to_all.15 = f32[2,1,46080]{2,1,0:T(1,128)S(1)} all-to-all(f32[2,1,46080]{2,1,0:T(1,128)S(1)} %reshape.4799), channel_id=1, replica_groups=mesh['pts'=64,'grp'=2] {'grp'}, dimensions={0} | all-to-all | bytes 737280 | tf_op jit(solution)/shard_map/all_to_all | solution.py:19
  205.5 1.8 reduce.4
  208.7 20.0 %all_to_all.16 = f32[64,1,720]{2,1,0:T(1,128)S(1)} all-to-all(f32[64,1,720]{2,1,0:T(1,128)S(1)} %reshape.4801), channel_id=1, replica_groups=mesh['pts'=64,'grp'=2] {'pts'}, dimensions={0} | all-to-all | bytes 368640 | tf_op jit(solution)/shard_map/all_to_all | solution.py:19
  238.9 2.1 reshape.4803
  241.0 5.3 %all-to-all-start.2 = ((f32[128,1,720]{2,1,0:T(1,128)}), f32[128,1,720]{2,1,0:T(1,128)S(1)}, u32[]{:S(2)}, u32[]{:S(2)}) async-start(f32[128,1,720]{2,1,0:T(1,128)} %reshape.4803), calls=%async_computation.2 | async-start | bytes 786432 | tf_op jit(solution)/shard_map/all_to_all | solution.py:207
  247.4 11.1 %all-to-all-done.2 = f32[128,1,720]{2,1,0:T(1,128)S(1)} async-done(((f32[128,1,720]{2,1,0:T(1,128)}), f32[128,1,720]{2,1,0:T(1,128)S(1)}, u32[]{:S(2)}, u32[]{:S(2)}) %all-to-all-start.2) | async-done | bytes 368672 | tf_op jit(solution)/shard_map/all_to_all | solution.py:207
  261.1 55.7 %while.43 = (s32[]{:T(128)}, f32[16,45,512]{2,1,0:T(8,128)}, s32[16,512]{1,0:T(8,128)}, s32[2048]{0:T(1024)S(1)}, f32[45,2048]{1,0:T(8,128)S(1)}, /*index=5*/s32[]{:T(128)}) while((s32[]{:T(128)}, f32[16,45,512]{2,1,0:T(8,128)}, s32[16,512]{1,0:T(8,128)}, s32[2048]{0:T(1024)S(1)}, f32[45,2048]{1,0:T(8,128)S(1)}, /*index=5*/s32[]{:T(128)}) %tuple.423), condition=%wide.region_10.11_spmd, body=%wide.region_9.10_spmd.sunk | while | flops 567279616 | bytes 481365 | solution.py:213
  261.9 2.8 fusion.85
  265.4 2.8 fusion.85
  268.8 2.7 fusion.85
  272.3 2.7 fusion.85
  275.8 2.8 fusion.85
  279.3 2.8 fusion.85
  282.8 2.8 fusion.85
  286.2 2.8 fusion.85
  289.7 2.8 fusion.85
  293.2 2.8 fusion.85
  296.7 2.8 fusion.85
  300.2 2.8 fusion.85
  303.6 2.8 fusion.85
  307.1 2.7 fusion.85
  310.6 2.8 fusion.85
  314.1 2.8 fusion.85
  316.8 1.8 fusion.68
  318.6 3.6 %fusion.67 = (f32[1,16,512]{2,0,1:T(1,128)S(1)}, f32[1,16,512]{2,0,1:T(1,128)S(1)}, f32[1,16,512]{2,0,1:T(1,128)S(1)}, f32[1,16,512]{2,0,1:T(1,128)S(1)}, f32[1,...) fusion(f32[45,16,512]{2,0,1:T(8,128)} %bitcast.185), kind=kLoop, calls=%fused_computation.289 | loop fusion | bytes 1245184 | tf_op jit(solution)/shard_map/slice | solution.py:172
  322.2 3.6 %fusion.66 = (f32[1,16,512]{2,0,1:T(1,128)S(1)}, f32[1,16,512]{2,0,1:T(1,128)S(1)}, f32[1,16,512]{2,0,1:T(1,128)S(1)}, f32[1,16,512]{2,0,1:T(1,128)S(1)}, f32[1,...) fusion(f32[45,16,512]{2,0,1:T(8,128)} %bitcast.186), kind=kLoop, calls=%fused_computation.288 | loop fusion | bytes 1245184 | tf_op jit(solution)/shard_map/slice | solution.py:172
  328.4 1.8 stack.182
  (324 shorter events, 124.8 us)
Async XLA Ops:
  74.4 63.3 %copy-start = (f32[18,8192]{1,0:T(8,128)S(1)}, f32[18,8192]{1,0:T(8,128)}, u32[]{:S(2)}) copy-start(f32[18,8192]{1,0:T(8,128)} %param.14) | copy-start | bytes 1769476
  74.4 63.2 %copy-start.1 = (f32[6,8192]{1,0:T(8,128)S(1)}, f32[6,8192]{1,0:T(8,128)}, u32[]{:S(2)}) copy-start(f32[6,8192]{1,0:T(8,128)} %param.15) | copy-start | bytes 589828
  136.8 2.5 copy-start.7
  136.8 2.5 copy-start.6
  238.8 7.5 %copy-start.2 = (f32[2,8192]{1,0:T(2,128)S(1)}, f32[2,8192]{1,0:T(2,128)}, u32[]{:S(2)}) copy-start(f32[2,8192]{1,0:T(2,128)} %param.16) | copy-start | bytes 196612
  238.8 7.5 %copy-start.3 = (f32[1,16,512]{2,0,1:T(1,128)S(1)}, f32[1,16,512]{2,0,1:T(1,128)}, u32[]{:S(2)}) copy-start(f32[1,16,512]{2,0,1:T(1,128)} %get-tuple-element.485) | copy-start | bytes 98308
  238.8 7.5 %copy-start.4 = (f32[1,16,512]{2,0,1:T(1,128)S(1)}, f32[1,16,512]{2,0,1:T(1,128)}, u32[]{:S(2)}) copy-start(f32[1,16,512]{2,0,1:T(1,128)} %get-tuple-element.486) | copy-start | bytes 98308
  238.8 7.5 %copy-start.5 = (f32[1,16,512]{2,0,1:T(1,128)S(1)}, f32[1,16,512]{2,0,1:T(1,128)}, u32[]{:S(2)}) copy-start(f32[1,16,512]{2,0,1:T(1,128)} %get-tuple-element.487) | copy-start | bytes 98308
  241.0 17.5 %all-to-all-start.2 = ((f32[128,1,720]{2,1,0:T(1,128)}), f32[128,1,720]{2,1,0:T(1,128)S(1)}, u32[]{:S(2)}, u32[]{:S(2)}) async-start(f32[128,1,720]{2,1,0:T(1,128)} %reshape.4803), calls=%async_computation.2 | async-start | bytes 786432 | tf_op jit(solution)/shard_map/all_to_all | solution.py:207
